TPU v7x, 32 devices: a whole 2x2x4 slice. The times are simulated.
32 devices in a mesh: groups: 2 (over x), blk: 4 (over y, core), col: 4 (over z).
Axes of the slice: x: 2, y: 2, z: 4, core: 2. Of those that a mesh axis runs over, the one named last changes fastest.
Arguments:
- pair_block: bfloat16 [4096, 16384], P(('groups', 'blk'), 'col'), parts along dimension 0, may hold values from -1.5 to 1.5
- occ_energy: float32 [2], P('groups'), parts along dimension 0, may hold values from -1.5 to -0.3
- virt_energy: float32 [4096], P('groups'), parts along dimension 0, may hold values from 0.2 to 3
- frequency: float32 [2], P('groups'), parts along dimension 0, may hold values from 0.2 to 2
Outputs:
- dielectric: float32 [32768, 16384], P(('groups', 'col'), 'blk'), parts along dimension 0
There are 2 independent parts, one for each index of `groups`. A program takes and returns all parts, laid end to end along the dimension named above; each array names one. Nothing has to cross between parts.
All inputs are finite; a program needn't handle non-finite values.
Results may differ from a plain program's by a relative error of at most 0.0027.
Values may be sent and summed in bfloat16 or wider, within the bound.
No kernel may reach another device: no remote copies, remote signals or barrier semaphores. Data moves between devices by JAX's collectives and lax.ppermute only.
A program may use at most 192 MiB of HBM per device.

v0:
```python
import jax
import jax.numpy as jnp
from jax import lax
from jax.sharding import PartitionSpec as P


def pair_weights(occ_energy, virt_energy, frequency):
    gap = (virt_energy[None, :] - occ_energy[:, None]).reshape(-1)
    return 2.0 * gap / (gap * gap + frequency[0] * frequency[0])


def shards(pair_block, occ_energy, virt_energy, frequency):
    weights = pair_weights(occ_energy, virt_energy, frequency)
    row_full = lax.all_gather(pair_block, "col", axis=1, tiled=True)
    column_slab = lax.all_to_all(row_full, "blk", split_axis=1, concat_axis=0, tiled=True)
    scaled = (
        lax.all_gather(pair_block, "blk", axis=0, tiled=True).astype(jnp.float32) * weights[:, None]
    ).astype(jnp.bfloat16)
    return lax.dot_general(
        scaled, column_slab, (((0,), (0,)), ((), ())), preferred_element_type=jnp.float32
    )


def solution(mesh):
    return jax.shard_map(
        shards,
        mesh=mesh,
        in_specs=(P(("groups", "blk"), "col"), P("groups"), P("groups"), P("groups")),
        out_specs=P(("groups", "col"), "blk"),
        check_vma=False,
    )
```

profile of v0, /device:TPU:0, one launch (start us, length us, event | category | flops | bytes accessed | tf_op | source)
XLA Modules:
  0.0 691.5 jit_solution(8358652491445676149)
XLA Ops:
  6.5 0.0 all-gather.5.cloned.1.call-start
  6.5 6.4 copy.5
  12.9 0.0 all-gather.5.cloned.1.call-update
  13.0 0.0 all-gather.3.cloned.1.call-start
  13.0 0.7 all-gather.3.cloned.1.call-update
  13.7 288.9 %all-gather.5.cloned.1.call-done = bf16[512,16384]{0,1:T(8,128)(2,1)} async-done(((bf16[512,4096]{0,1:T(8,128)(2,1)}), bf16[512,16384]{0,1:T(8,128)(2,1)}) %all-gather.5.cloned.1.call-update) | async-done | bytes 16777232 | tf_op jit(solution)/shard_map/all_gather | solution.py:14
  302.6 0.0 copy-start
  302.6 7.3 %all-to-all-start = ((bf16[512,4,4096]{0,2,1:T(8,128)(2,1)}), bf16[512,4,4096]{0,2,1:T(8,128)(2,1)}, u32[]{:S(2)}, u32[]{:S(2)}) async-start(bf16[512,4,4096]{0,2,1:T(8,128)(2,1)} %bitcast.8), calls=%async_computation | async-start | bytes 33554432 | tf_op jit(solution)/shard_map/all_to_all | solution.py:15
  311.2 0.0 copy-done
  311.2 271.6 %all-to-all-done = bf16[512,4,4096]{0,2,1:T(8,128)(2,1)} async-done(((bf16[512,4,4096]{0,2,1:T(8,128)(2,1)}), bf16[512,4,4096]{0,2,1:T(8,128)(2,1)}, u32[]{:S(2)}, u32[]{:S(2)}) %all-to-all-start) | async-done | bytes 16777248 | tf_op jit(solution)/shard_map/all_to_all | solution.py:15
  582.8 20.7 %copy.6 = bf16[4,512,4096]{2,1,0:T(8,128)(2,1)} copy(bf16[4,512,4096]{1,2,0:T(8,128)(2,1)} %bitcast.3) | data formatting | bytes 33554432 | tf_op jit(solution)/shard_map/all_to_all | solution.py:15
  603.5 0.0 all-gather.3.cloned.1.call-done
  603.5 81.2 %fusion = f32[4096,4096]{1,0:T(8,128)} fusion(bf16[2048,4096]{1,0:T(8,128)(2,1)} %bitcast.9, bf16[2048,4096]{1,0:T(8,128)(2,1)} %all-gather.3.cloned.1.call-done, f32[2048]{0:T(1024)S(1)} %add_divide_fusion), kind=kOutput, calls=%fused_computation.1 | convolution fusion | flops 68744642560 | bytes 100671488 | tf_op jit(solution)/shard_map/dot_general | solution.py:19
  (1 shorter events, 0.0 us)
Async XLA Ops:
  6.5 296.1 %all-gather.5.cloned.1.call-start = ((), (), s32[]{:S(2)}) async-start(), calls=%async_computation.2 | async-start | bytes 20971520 | tf_op jit(solution)/shard_map/all_gather | solution.py:14
  13.0 590.5 %all-gather.3.cloned.1.call-start = ((), (), s32[]{:S(2)}) async-start(), calls=%async_computation.1 | async-start | bytes 20971520 | tf_op jit(solution)/shard_map/all_gather | solution.py:17
  302.6 8.6 %copy-start = (f32[2048]{0:T(1024)S(1)}, f32[2048]{0:T(1024)}, u32[]{:S(2)}) copy-start(f32[2048]{0:T(1024)} %param.6) | copy-start | bytes 24580
  302.6 280.2 %all-to-all-start = ((bf16[512,4,4096]{0,2,1:T(8,128)(2,1)}), bf16[512,4,4096]{0,2,1:T(8,128)(2,1)}, u32[]{:S(2)}, u32[]{:S(2)}) async-start(bf16[512,4,4096]{0,2,1:T(8,128)(2,1)} %bitcast.8), calls=%async_computation | async-start | bytes 33554432 | tf_op jit(solution)/shard_map/all_to_all | solution.py:15
Sparse Core Ops, SparseCore 0:
  13.1 289.4 all-gather.4
  304.2 194.0 all-gather.2
where the time goes:
time: 692 us; the launch traced here: 691 us
  waiting for transfers between devices  561 us (81%)
  matrix products  81.2 us (12%)
  local copies, waits for them, and re-layouts  27.1 us (4%)
  between operations  14.7 us (2%)
  starting transfers between devices  7.3 us (1%)
    all_gather x1, waiting for transfers between devices, shards(): row_full = lax.all_gather(pair_block, 'col', axis=1, tiled=True)  289 us
    all_to_all x1, waiting for transfers between devices, shards(): lax.all_to_all(row_full, 'blk', split_axis=1, concat_axis=0, tiled=True)  272 us
    dot_general x1, matrix products, shards(): lax.dot_general(scaled, column_slab, (((0,), (0,)), ((), ())), preferred_...  81.2 us
    all_to_all x1, local copies, waits for them, and re-layouts, shards(): lax.all_to_all(row_full, 'blk', split_axis=1, concat_axis=0, tiled=True)  20.7 us
  transfers between devices with their start and end apart: 3, of which 2 were waited for; matrix products, arithmetic and copies ran while one was open for 3% of the time, Pallas kernels for 0%

commit v1 on v0

--- a/solution.py
+++ b/solution.py
@@ -11,7 +11,7 @@
 
 def shards(pair_block, occ_energy, virt_energy, frequency):
     weights = pair_weights(occ_energy, virt_energy, frequency)
-    row_full = lax.all_gather(pair_block, "col", axis=1, tiled=True)
+    row_full = jnp.concatenate(lax.all_gather(pair_block, "col"), axis=1)
     column_slab = lax.all_to_all(row_full, "blk", split_axis=1, concat_axis=0, tiled=True)
     scaled = (
         lax.all_gather(pair_block, "blk", axis=0, tiled=True).astype(jnp.float32) * weights[:, None]

time: 692 us -> 667 us (0.964)
  local copies, waits for them, and re-layouts: 27.1 us -> 0.01 us
    all_to_all x1, waiting for transfers between devices: 272 us -> 84.5 us  [shards(): lax.all_to_all(row_full, 'blk', split_axis=1, concat_axis=0, tiled=True)]
    all_gather x1, waiting for transfers between devices: 0.01 us -> 187 us  [shards(): lax.all_gather(pair_block, 'blk', axis=0, tiled=True).astype(jnp.float32)]
    all_to_all x1 -> x0, local copies, waits for them, and re-layouts: 20.7 us -> none  [shards(): lax.all_to_all(row_full, 'blk', split_axis=1, concat_axis=0, tiled=True)]
  transfers between devices with their start and end apart: 3 -> 3, of which waited for: 2 -> 3; matrix products, arithmetic and copies ran while one was open for 3% -> 0% of each run, Pallas kernels for 0% -> 0%
where the time goes in v1:
time: 667 us
  waiting for transfers between devices  563 us (84%)
  matrix products  81.1 us (12%)
  between operations  14.7 us (2%)
  starting transfers between devices  7.3 us (1%)
    all_gather x1, waiting for transfers between devices, shards(): row_full = jnp.concatenate(lax.all_gather(pair_block, 'col'), axis=1)  290 us
    all_gather x1, waiting for transfers between devices, shards(): lax.all_gather(pair_block, 'blk', axis=0, tiled=True).astype(jnp.float32)  187 us
    all_to_all x1, waiting for transfers between devices, shards(): lax.all_to_all(row_full, 'blk', split_axis=1, concat_axis=0, tiled=True)  84.5 us
    dot_general x1, matrix products, shards(): lax.dot_general(scaled, column_slab, (((0,), (0,)), ((), ())), preferred_...  81.1 us
  transfers between devices with their start and end apart: 3, of which 3 were waited for; matrix products, arithmetic and copies ran while one was open for 0% of the time, Pallas kernels for 0%

profile of v1, /device:TPU:0, one launch (start us, length us, event | category | flops | bytes accessed | tf_op | source)
XLA Modules:
  0.0 666.6 jit_solution(17955778352746648957)
XLA Ops:
  6.5 0.0 all-gather.6.cloned.1.call-start
  6.5 0.7 all-gather.6.cloned.1.call-update
  7.3 0.0 all-gather.4.cloned.1.call-start
  7.3 0.7 all-gather.4.cloned.1.call-update
  8.0 290.4 %all-gather.6.cloned.1.call-done = bf16[2048,4096]{1,0:T(8,128)(2,1)} async-done(((bf16[512,4096]{1,0:T(8,128)(2,1)}), bf16[2048,4096]{1,0:T(8,128)(2,1)}) %all-gather.6.cloned.1.call-update) | async-done | bytes 16777232 | tf_op jit(solution)/shard_map/all_gather | solution.py:14
  298.4 0.0 copy-start
  298.4 7.3 %all-to-all-start = ((bf16[512,4,4096]{2,0,1:T(8,128)(2,1)}), bf16[512,4,4096]{2,0,1:T(8,128)(2,1)}, u32[]{:S(2)}, u32[]{:S(2)}) async-start(bf16[512,4,4096]{2,0,1:T(8,128)(2,1)} %bitcast.11), calls=%async_computation | async-start | bytes 33554432 | tf_op jit(solution)/shard_map/all_to_all | solution.py:15
  307.0 0.0 copy-done
  307.0 187.1 %all-gather.4.cloned.1.call-done = bf16[2048,4096]{1,0:T(8,128)(2,1)} async-done(((bf16[512,4096]{1,0:T(8,128)(2,1)}), bf16[2048,4096]{1,0:T(8,128)(2,1)}) %all-gather.4.cloned.1.call-update) | async-done | bytes 16777232 | tf_op jit(solution)/shard_map/all_gather | solution.py:17
  494.1 84.5 %all-to-all-done = bf16[512,4,4096]{2,0,1:T(8,128)(2,1)} async-done(((bf16[512,4,4096]{2,0,1:T(8,128)(2,1)}), bf16[512,4,4096]{2,0,1:T(8,128)(2,1)}, u32[]{:S(2)}, u32[]{:S(2)}) %all-to-all-start) | async-done | bytes 16777248 | tf_op jit(solution)/shard_map/all_to_all | solution.py:15
  578.6 81.1 %fusion = f32[4096,4096]{1,0:T(8,128)} fusion(bf16[2048,4096]{1,0:T(8,128)(2,1)} %bitcast.5, bf16[2048,4096]{1,0:T(8,128)(2,1)} %all-gather.4.cloned.1.call-done, f32[2048]{0:T(1024)S(1)} %add_divide_fusion), kind=kOutput, calls=%fused_computation.1 | convolution fusion | flops 68744642560 | bytes 100671488 | tf_op jit(solution)/shard_map/dot_general | solution.py:19
  (1 shorter events, 0.0 us)
Async XLA Ops:
  6.5 291.9 %all-gather.6.cloned.1.call-start = ((), (), s32[]{:S(2)}) async-start(), calls=%async_computation.2 | async-start | bytes 20971520 | tf_op jit(solution)/shard_map/all_gather | solution.py:14
  7.3 486.8 %all-gather.4.cloned.1.call-start = ((), (), s32[]{:S(2)}) async-start(), calls=%async_computation.1 | async-start | bytes 20971520 | tf_op jit(solution)/shard_map/all_gather | solution.py:17
  298.4 8.6 %copy-start = (f32[2048]{0:T(1024)S(1)}, f32[2048]{0:T(1024)}, u32[]{:S(2)}) copy-start(f32[2048]{0:T(1024)} %param.6) | copy-start | bytes 24580
  298.4 280.2 %all-to-all-start = ((bf16[512,4,4096]{2,0,1:T(8,128)(2,1)}), bf16[512,4,4096]{2,0,1:T(8,128)(2,1)}, u32[]{:S(2)}, u32[]{:S(2)}) async-start(bf16[512,4,4096]{2,0,1:T(8,128)(2,1)} %bitcast.11), calls=%async_computation | async-start | bytes 33554432 | tf_op jit(solution)/shard_map/all_to_all | solution.py:15
Sparse Core Ops, SparseCore 0:
  8.9 289.4 all-gather.5
  300.0 194.0 all-gather.3

commit v2 on v0

--- a/solution.py
+++ b/solution.py
@@ -12,7 +12,10 @@
 def shards(pair_block, occ_energy, virt_energy, frequency):
     weights = pair_weights(occ_energy, virt_energy, frequency)
     row_full = lax.all_gather(pair_block, "col", axis=1, tiled=True)
-    column_slab = lax.all_to_all(row_full, "blk", split_axis=1, concat_axis=0, tiled=True)
+    column_slab = jnp.concatenate(
+        lax.all_to_all(jnp.stack(jnp.split(row_full, lax.axis_size("blk"), axis=1)), "blk", 0, 0),
+        axis=0,
+    )
     scaled = (
         lax.all_gather(pair_block, "blk", axis=0, tiled=True).astype(jnp.float32) * weights[:, None]
     ).astype(jnp.bfloat16)

time: 692 us -> 670 us (0.968)
  local copies, waits for them, and re-layouts: 27.1 us -> 6.61 us
  waiting for transfers between devices: 561 us -> 551 us
  other arithmetic: 0.01 us -> 8.76 us
    all_to_all x1, waiting for transfers between devices: 272 us -> 100 us  [shards(): lax.all_to_all(jnp.stack(jnp.split(row_full, lax.axis_size('blk'), axis=1...]
    all_gather x1, waiting for transfers between devices: 0.01 us -> 159 us  [shards(): lax.all_gather(pair_block, 'blk', axis=0, tiled=True).astype(jnp.float32)]
    all_to_all x1 -> x0, local copies, waits for them, and re-layouts: 20.7 us -> none  [shards(): lax.all_to_all(row_full, 'blk', split_axis=1, concat_axis=0, tiled=True)]
    another operation x0 -> x1, other arithmetic: none -> 8.75 us  [shards(): jnp.stack(jnp.split(row_full, lax.axis_size('blk'), axis=1))]
  transfers between devices with their start and end apart: 3 -> 3, of which waited for: 2 -> 3; matrix products, arithmetic and copies ran while one was open for 3% -> 2% of each run, Pallas kernels for 0% -> 0%
where the time goes in v2:
time: 670 us
  waiting for transfers between devices  551 us (82%)
  matrix products  81.2 us (12%)
  between operations  14.7 us (2%)
  other arithmetic  8.76 us (1%)
  starting transfers between devices  7.48 us (1%)
    all_gather x1, waiting for transfers between devices, shards(): row_full = lax.all_gather(pair_block, 'col', axis=1, tiled=True)  290 us
    all_gather x1, waiting for transfers between devices, shards(): lax.all_gather(pair_block, 'blk', axis=0, tiled=True).astype(jnp.float32)  159 us
    all_to_all x1, waiting for transfers between devices, shards(): lax.all_to_all(jnp.stack(jnp.split(row_full, lax.axis_size('blk'), axis=1...  100 us
    dot_general x1, matrix products, shards(): lax.dot_general(scaled, column_slab, (((0,), (0,)), ((), ())), preferred_...  81.2 us
  transfers between devices with their start and end apart: 3, of which 3 were waited for; matrix products, arithmetic and copies ran while one was open for 2% of the time, Pallas kernels for 0%

profile of v2, /device:TPU:0, one launch (start us, length us, event | category | flops | bytes accessed | tf_op | source)
XLA Modules:
  0.0 669.8 jit_solution(16342548784936701926)
XLA Ops:
  6.5 0.0 all-gather.5.cloned.1.call-start
  6.5 0.7 all-gather.5.cloned.1.call-update
  7.3 0.0 all-gather.3.cloned.1.call-start
  7.3 0.7 all-gather.3.cloned.1.call-update
  8.0 290.4 %all-gather.5.cloned.1.call-done = bf16[512,16384]{1,0:T(8,128)(2,1)} async-done(((bf16[512,4096]{1,0:T(8,128)(2,1)}), bf16[512,16384]{1,0:T(8,128)(2,1)}) %all-gather.5.cloned.1.call-update) | async-done | bytes 16777232 | tf_op jit(solution)/shard_map/all_gather | solution.py:14
  298.4 6.6 slice_bitcast_fusion.3
  305.0 8.7 %pad_maximum_fusion = bf16[4,512,4096]{2,1,0:T(8,128)(2,1)} fusion(bf16[1,512,4096]{2,1,0:T(8,128)(2,1)S(1)} %get-tuple-element.6, bf16[1,512,4096]{2,1,0:T(8,128)(2,1)S(1)} %get-tuple-element.7, bf16[1,512,4096]{2,1,0:T(8,128)(2,1)S(1)} %get-tuple-element.8, bf16[1,512,4096]{2,1,0:T(8,128)(2,1)S(1)} %get-tuple-element.5), kind=kLoop, calls=%fused_computation.2 | loop fusion | flops 25165824 | bytes 33554432 | tf_op jit(solution)/shard_map/stack | solution.py:16
  313.8 0.0 copy-start
  313.8 7.4 %all-to-all-start = ((bf16[4,512,4096]{2,1,0:T(8,128)(2,1)}), bf16[4,512,4096]{2,1,0:T(8,128)(2,1)}, u32[]{:S(2)}, u32[]{:S(2)}) async-start(bf16[4,512,4096]{2,1,0:T(8,128)(2,1)} %pad_maximum_fusion), calls=%async_computation | async-start | bytes 33554432 | tf_op jit(solution)/shard_map/all_to_all | solution.py:16
  322.5 0.0 copy-done
  322.5 159.1 %all-gather.3.cloned.1.call-done = bf16[2048,4096]{1,0:T(8,128)(2,1)} async-done(((bf16[512,4096]{1,0:T(8,128)(2,1)}), bf16[2048,4096]{1,0:T(8,128)(2,1)}) %all-gather.3.cloned.1.call-update) | async-done | bytes 16777232 | tf_op jit(solution)/shard_map/all_gather | solution.py:20
  481.7 100.1 %all-to-all-done = bf16[4,512,4096]{2,1,0:T(8,128)(2,1)} async-done(((bf16[4,512,4096]{2,1,0:T(8,128)(2,1)}), bf16[4,512,4096]{2,1,0:T(8,128)(2,1)}, u32[]{:S(2)}, u32[]{:S(2)}) %all-to-all-start) | async-done | bytes 16777248 | tf_op jit(solution)/shard_map/all_to_all | solution.py:16
  581.8 81.2 %fusion = f32[4096,4096]{1,0:T(8,128)} fusion(bf16[2048,4096]{1,0:T(8,128)(2,1)} %bitcast.6, bf16[2048,4096]{1,0:T(8,128)(2,1)} %all-gather.3.cloned.1.call-done, f32[2048]{0:T(1024)S(1)} %add_divide_fusion), kind=kOutput, calls=%fused_computation.1 | convolution fusion | flops 68744642560 | bytes 100671488 | tf_op jit(solution)/shard_map/dot_general | solution.py:22
  (1 shorter events, 0.0 us)
Async XLA Ops:
  6.5 291.9 %all-gather.5.cloned.1.call-start = ((), (), s32[]{:S(2)}) async-start(), calls=%async_computation.2 | async-start | bytes 20971520 | tf_op jit(solution)/shard_map/all_gather | solution.py:14
  7.3 474.4 %all-gather.3.cloned.1.call-start = ((), (), s32[]{:S(2)}) async-start(), calls=%async_computation.1 | async-start | bytes 20971520 | tf_op jit(solution)/shard_map/all_gather | solution.py:20
  313.8 8.7 %copy-start = (f32[2048]{0:T(1024)S(1)}, f32[2048]{0:T(1024)}, u32[]{:S(2)}) copy-start(f32[2048]{0:T(1024)} %param.6) | copy-start | bytes 24580
  313.8 268.0 %all-to-all-start = ((bf16[4,512,4096]{2,1,0:T(8,128)(2,1)}), bf16[4,512,4096]{2,1,0:T(8,128)(2,1)}, u32[]{:S(2)}, u32[]{:S(2)}) async-start(bf16[4,512,4096]{2,1,0:T(8,128)(2,1)} %pad_maximum_fusion), calls=%async_computation | async-start | bytes 33554432 | tf_op jit(solution)/shard_map/all_to_all | solution.py:16
Sparse Core Ops, SparseCore 0:
  8.9 289.4 all-gather.4
  300.0 181.6 all-gather.2
